TPU v7x, 256 devices: a whole 4x4x8 slice. The times are simulated.
256 devices in a mesh: gx: 8 (over z), gy: 8 (over x, y_lo), gz: 4 (over y_hi, core).
Axes of the slice: x: 4, y: 4 (y_hi: 2, y_lo: 2; y = y_hi * 2 + y_lo), z: 8, core: 2. Of those that a mesh axis runs over, the one named last changes fastest.
Arguments:
- fields_now: float32 [24, 64, 64, 512], P(None, 'gx', 'gy', 'gz'), may hold values from -6 to 6
- parent: float32 [24, 64, 64, 512], P(None, 'gx', 'gy', 'gz'), may hold values from -6 to 6
- advect: float32 [3, 24, 24], replicated, may hold values from -0.75 to 0.75
- diffuse: float32 [3, 24, 24], replicated, may hold values from -0.25 to 0.25
- box_shift: int32 [3], replicated, may hold values from 1 to 4
Outputs:
- section_slope: float32 [24, 64, 64, 512], P(None, 'gx', 'gy', 'gz')
- section_value: float32 [24, 64, 64, 512], P(None, 'gx', 'gy', 'gz')
All inputs are finite; a program needn't handle non-finite values.
Results may differ from a plain program's by a relative error of at most 0.0001.
Values sent between devices are 32-bit elements; how exact they have to be, the bound alone decides.
A program may use at most 64 MiB of HBM per device.

v0:
```python
import jax
import jax.numpy as jnp
from jax import lax
from jax.experimental import pallas as pl
from jax.experimental.pallas import tpu as pltpu
from jax.sharding import PartitionSpec as P

MESH = pl.DeviceIdType.MESH
F32, BF16 = jnp.float32, jnp.bfloat16
GROUPS = 3
NX, NY, NZ = 8, 8, 128
REACH = 4
AXES = ("gx", "gy", "gz")
FACES = ((0, 0, 1), (0, 1, 0), (1, 0, 0))


def kernel(shift_hbm, now_hbm, parent_hbm, advect_hbm, diffuse_hbm, slope_v, value_v, *scratch):
    scratch = list(scratch)

    def take(count):
        got = scratch[:count]
        del scratch[:count]
        return got

    shift, advect, diffuse, now_v, parent_v, acc = take(6)
    mixed, mixed_y, weights_xz, weights_y, weight_f32, lanes_out, lanes_in, lanes = take(8)
    raw = [take(2) for _ in range(GROUPS)]
    moved, above, box = take(GROUPS), take(GROUPS), take(GROUPS)
    arm_out, arm_low, arm_high = take(GROUPS), take(GROUPS), take(GROUPS)
    load_sem, a_send, a_recv, b_send, b_recv, z_send, z_recv, arm_send, arm_recv = take(10)

    place = [lax.axis_index(axis) for axis in AXES]
    sizes = [lax.axis_size(axis) for axis in AXES]
    gx, gy, gz = place

    def exists(step):
        found = None
        for at, size, by in zip(place, sizes, step):
            if by:
                inside = (at < size - 1) if by > 0 else (at > 0)
                found = inside if found is None else found & inside
        return found

    def peer(step):
        return {axis: at + by for axis, at, by in zip(AXES, place, step) if by}

    def remote(src, dst, send, recv, step):
        return pltpu.make_async_remote_copy(
            src_ref=src, dst_ref=dst, send_sem=send, recv_sem=recv, device_id=peer(step), device_id_type=MESH)

    def opposite(step):
        return tuple(-by for by in step)

    barrier = pltpu.get_barrier_semaphore()
    steps = []
    for step in FACES + ((0, 1, 1),):
        steps += [step, opposite(step)]
    for step in steps:
        @pl.when(exists(step))
        def _():
            pl.semaphore_signal(barrier, inc=1, device_id=peer(step), device_id_type=MESH)

    loads = [pltpu.make_async_copy(now_hbm.at[pl.ds(8 * c, 8)], now_v.at[pl.ds(8 * c, 8)], load_sem.at[c])
             for c in range(GROUPS)]
    loads.append(pltpu.make_async_copy(shift_hbm, shift, load_sem.at[3]))
    loads.append(pltpu.make_async_copy(parent_hbm, parent_v, load_sem.at[4]))
    loads.append(pltpu.make_async_copy(advect_hbm, advect, load_sem.at[5]))
    loads.append(pltpu.make_async_copy(diffuse_hbm, diffuse, load_sem.at[6]))
    for load in loads:
        load.start()

    lane = lax.broadcasted_iota(jnp.int32, (8, NZ), 1)
    four, eight = lane // 4, lane // 8
    zero = jnp.zeros((8, NZ), F32)

    def turn(c, packed):
        loads[c].wait()
        for x in range(NX):
            tiles = jnp.swapaxes(now_v[8 * c:8 * c + 8, x], 0, 1)
            raw[c][x // 4][x % 4, 0:8] = tiles
            at = 3 * x + c
            packed = [jnp.where(four == at, pltpu.roll(tiles[y], 4 * at, 1), packed[y]) for y in range(NY)]
        return packed

    packed = turn(0, [zero] * NY)

    pl.semaphore_wait(barrier, sum(exists(step).astype(jnp.int32) for step in steps))

    lane_copies = [
        remote(lanes_out, lanes_in.at[0:8], z_send.at[0], z_recv.at[0], (0, 0, -1)),
        remote(lanes_out.at[0:REACH], lanes_in.at[8:8 + REACH], z_send.at[1], z_recv.at[1], (0, -1, -1)),
        remote(lanes.at[0], lanes.at[1], z_send.at[2], z_recv.at[2], (-1, 0, 0))]
    has_lanes = exists((0, 0, 1))
    lane_sent = [exists((0, 0, -1)), exists((0, -1, -1)), has_lanes & exists((-1, 0, 0))]
    lane_received = [has_lanes, exists((0, 1, 1)), has_lanes & exists((1, 0, 0))]
    a_copies = [[remote(raw[c][h].at[:, 0:REACH], raw[c][h].at[:, 8:8 + REACH],
                        a_send.at[c, h], a_recv.at[c, h], (0, -1, 0)) for h in range(2)] for c in range(GROUPS)]
    b_copies = [remote(moved[c].at[0:REACH], above[c], b_send.at[c], b_recv.at[c], (-1, 0, 0))
                for c in range(GROUPS)]
    def send_rows(c):
        @pl.when(exists((0, -1, 0)))
        def _():
            for h in range(2):
                a_copies[c][h].start()

    send_rows(0)
    for c in range(1, GROUPS):
        packed = turn(c, packed)
    for y in range(NY):
        lanes_out[y] = packed[y]
    for k in range(2):
        @pl.when(lane_sent[k])
        def _():
            lane_copies[k].start()
    for c in range(1, GROUPS):
        send_rows(c)

    edges = (
        ((-1, 0, 0), lambda c: box[c].at[0:3, 3:11]), ((1, 0, 0), lambda c: box[c].at[11:14, 3:11]),
        ((0, -1, 0), lambda c: box[c].at[3:11, 0:3]), ((0, 1, 0), lambda c: box[c].at[3:11, 11:14]),
        ((0, 0, -1), lambda c: arm_low[c]), ((0, 0, 1), lambda c: arm_high[c]))
    for step, view in edges:
        @pl.when(jnp.logical_not(exists(step)))
        def _():
            for c in range(GROUPS):
                ref = view(c)
                ref[...] = jnp.zeros(ref.shape, F32)

    loads[5].wait()
    loads[6].wait()
    for c in range(GROUPS):
        for k, q in enumerate((0, 2, 3, 5) * 2 + (1, 4) * 2):
            source, scale = (advect, 8.0 / 12.0) if q < 3 else (diffuse, 16.0 / 12.0)
            weight_f32[:, 8 * k:8 * k + 8] = source[q % 3, :, 8 * c:8 * c + 8] * scale
        full = weight_f32[...]
        high = full.astype(BF16).astype(F32)
        both = jnp.concatenate([high, full - high], axis=0).astype(BF16)
        weights_xz[c] = both[:, 0:64]
        weights_y[c] = both[:, 64:96]
    loads[3].wait()
    loads[4].wait()
    s0, s1, s2 = shift[0], shift[1], shift[2]

    def arm(c, k, src, dst, step):
        return remote(src, dst, arm_send.at[c, k], arm_recv.at[c, k], step)

    def arms_of(c, h):
        xs = slice(3 + 4 * h, 7 + 4 * h)
        pair = slice(2 * h, 2 * h + 2)
        found = [
            (arm(c, 5 * h + 0, box[c].at[xs, 3:6], box[c].at[xs, 11:14], (0, -1, 0)), (0, -1, 0)),
            (arm(c, 5 * h + 1, box[c].at[xs, 8:11], box[c].at[xs, 0:3], (0, 1, 0)), (0, 1, 0)),
            (arm(c, 5 * h + 2, arm_out[c].at[pair], arm_high[c].at[pair], (0, 0, -1)), (0, 0, -1)),
            (arm(c, 5 * h + 3, arm_out[c].at[pair], arm_low[c].at[pair], (0, 0, 1)), (0, 0, 1))]
        if h == 0:
            found.append((arm(c, 4, box[c].at[3:6, 3:11], box[c].at[11:14, 3:11], (-1, 0, 0)), (-1, 0, 0)))
        else:
            found.append((arm(c, 9, box[c].at[8:11, 3:11], box[c].at[0:3, 3:11], (1, 0, 0)), (1, 0, 0)))
        return found

    arms = [[arms_of(c, h) for h in range(2)] for c in range(GROUPS)]

    def send_arms(some):
        for copy, step in some:
            @pl.when(exists(step))
            def _():
                copy.start()

    def build(c, h):
        for pair in range(2):
            packed = zero
            for x2 in range(2):
                x = 4 * h + 2 * pair + x2
                parent_tiles = jnp.swapaxes(parent_v[8 * c:8 * c + 8, x], 0, 1)
                old = x + s0
                if h == 0:
                    part, at_lane = 0, 4 * (3 * old + c)
                else:
                    here = old < NX
                    part = jnp.where(here, 0, 1)
                    at_lane = 4 * (3 * jnp.where(here, old, old - NX) + c)
                    own_at, above_at = jnp.minimum(old, NX - 1), jnp.maximum(old - NX, 0)
                in_x = gx * NX + old < sizes[0] * NX
                back = lax.rem(2 * NZ - s2 - at_lane, NZ)
                for y in range(NY):
                    if h == 0:
                        own = moved[c][old, y]
                    else:
                        own = jnp.where(here, moved[c][own_at, y], above[c][above_at, y])
                    tile = jnp.where(lane < NZ - s2, pltpu.roll(own, NZ - s2, 1),
                                     pltpu.roll(lanes[part, y], back, 1))
                    inside = in_x & (gy * NY + y + s1 < sizes[1] * NY)
                    limit = jnp.where(inside, sizes[2] * NZ - gz * NZ - s2, 0)
                    tile = jnp.where(lane < limit, tile, parent_tiles[y])
                    box[c][3 + x, 3 + y] = tile
                    at = 8 * x2 + y
                    packed = jnp.where(eight == at, pltpu.roll(tile, (8 * at + 4) % NZ, 1), packed)
            arm_out[c][2 * h + pair] = packed
        send_arms(arms[c][h][2:4] + arms[c][h][0:2])

    def shift_y(c, h):
        for x in range(4):
            for y in range(NY):
                moved[c][4 * h + x, y] = raw[c][h][x, y + s1]

    def take_rows(c, h):
        @pl.when(exists((0, 1, 0)))
        def _():
            a_copies[c][h].wait_recv()
        shift_y(c, h)

    def send_layers(c):
        take_rows(c, 0)

        @pl.when(exists((-1, 0, 0)))
        def _():
            b_copies[c].start()

    send_layers(0)
    take_rows(0, 1)
    for k in range(2):
        @pl.when(lane_received[k])
        def _():
            lane_copies[k].wait_recv()
    for y in range(NY):
        lanes[0, y] = lanes_in[y + s1]

    @pl.when(lane_sent[2])
    def _():
        lane_copies[2].start()
    build(0, 0)
    for c in range(1, GROUPS):
        send_layers(c)
        take_rows(c, 1)
        build(c, 0)

    for c in range(GROUPS):
        send_arms(arms[c][0][4:])

    @pl.when(lane_received[2])
    def _():
        lane_copies[2].wait_recv()
    for c in range(GROUPS):
        @pl.when(exists((1, 0, 0)))
        def _():
            b_copies[c].wait_recv()
        build(c, 1)
        send_arms(arms[c][1][4:])

    def line(m3, m2, m1, middle, p1, p2, p3):
        t1, t2, t3 = p1 + m1, p2 + m2, p3 + m3
        first = (p1 - m1) - 0.125 * (p2 - m2)
        second = (t1 - 0.0625 * t2) - middle
        return first, second, t1, t2, t3

    def sixth(t1, t2, t3):
        return ((15.0 / 64.0) * t1 - (6.0 / 64.0) * t2) + (1.0 / 64.0) * t3

    def put(ref, slot, y, parts):
        full = jnp.concatenate(parts, axis=0)
        rows = full.shape[0]
        top = full.astype(BF16)
        ref[slot, 0:rows, 128 * y:128 * y + 128] = top
        ref[slot, rows:2 * rows, 128 * y:128 * y + 128] = (full - top.astype(F32)).astype(BF16)

    def mix(weights, ref, slot):
        product = jnp.dot(weights, ref[slot], preferred_element_type=F32)
        return product[0:24] + product[24:48]

    def along_xz(c, x, h, pair, x2, slot):
        ends_pack = jnp.where(lane % 8 < 4, arm_low[c][2 * h + pair], arm_high[c][2 * h + pair])
        for y in range(NY):
            at = 8 * x2 + y
            u0 = box[c][3 + x, 3 + y]
            ends = pltpu.roll(ends_pack, (2 * NZ - 8 * at - 4) % NZ, 1)
            before = [pltpu.roll(jnp.where(lane >= NZ - o, ends, u0), o, 1) for o in (3, 2, 1)]
            after = [pltpu.roll(jnp.where(lane < o, ends, u0), NZ - o, 1) for o in (1, 2, 3)]
            middle = 1.875 * u0
            fz, sz, *tz = line(*before, middle, *after)
            fx, sx, *tx = line(*[box[c][x + o, 3 + y] for o in range(3)], middle,
                               *[box[c][x + o, 3 + y] for o in range(4, 7)])
            slope_v[8 * c + y, x] = sixth(*[i + k for i, k in zip(tx, tz)]) - (60.0 / 64.0) * u0
            put(mixed, slot, y, [fx, fz, sx, sz])
        product = mix(weights_xz[c], mixed, slot)
        acc[x] = product if c == 0 else acc[x] + product

    def along_y(c, x, slot):
        column = [box[c][3 + x, y] for y in range(14)]
        smooths = []
        for y in range(NY):
            fy, sy, *ty = line(*column[y:y + 3], 1.875 * column[3 + y], *column[y + 4:y + 7])
            smooths.append(slope_v[8 * c + y, x] + sixth(*ty))
            put(mixed_y, slot, y, [fy, sy])
        product = acc[x] + mix(weights_y[c], mixed_y, slot)
        if c < GROUPS - 1:
            for y in range(NY):
                slope_v[8 * c + y, x] = smooths[y]
            acc[x] = product
            return
        factors = [1.0 + 0.25 * jnp.tanh(box[0][3 + x, 3 + y][0:1]) for y in range(NY)]
        for g in range(GROUPS):
            slopes, values = [], []
            for y in range(NY):
                smooth = smooths[y] if g == c else slope_v[8 * g + y, x]
                slope = factors[y] * product[8 * g:8 * g + 8, 128 * y:128 * y + 128] + smooth
                slopes.append(slope)
                values.append(box[g][3 + x, 3 + y] + 0.125 * slope)
            slope_v[8 * g:8 * g + 8, x] = jnp.swapaxes(jnp.stack(slopes), 0, 1)
            value_v[8 * g:8 * g + 8, x] = jnp.swapaxes(jnp.stack(values), 0, 1)

    def wait_arms(c, which):
        for h, k in which:
            copy, step = arms[c][h][k]

            @pl.when(exists(opposite(step)))
            def _():
                copy.wait_recv()

    needs_xz = ([(0, 2), (0, 3), (1, 4)], [(1, 2), (1, 3), (0, 4)])
    for axis, c, h in (("xz", 0, 0), ("xz", 1, 0), ("xz", 2, 0), ("y", 0, 0), ("y", 1, 0), ("xz", 0, 1), ("xz", 1, 1),
                       ("xz", 2, 1), ("y", 2, 0), ("y", 0, 1), ("y", 1, 1), ("y", 2, 1)):
        wait_arms(c, needs_xz[h] if axis == "xz" else [(h, 0), (h, 1)])
        for x4 in range(4):
            if axis == "xz":
                along_xz(c, 4 * h + x4, h, x4 // 2, x4 % 2, x4)
            else:
                along_y(c, 4 * h + x4, x4)

    for copy, sent in zip(lane_copies, lane_sent):
        @pl.when(sent)
        def _():
            copy.wait_send()

    @pl.when(exists((0, -1, 0)))
    def _():
        for c in range(GROUPS):
            for h in range(2):
                a_copies[c][h].wait_send()

    @pl.when(exists((-1, 0, 0)))
    def _():
        for c in range(GROUPS):
            b_copies[c].wait_send()
    for c in range(GROUPS):
        for h in range(2):
            for copy, step in arms[c][h]:
                @pl.when(exists(step))
                def _():
                    copy.wait_send()


def section(fields_now, parent, advect, diffuse, box_shift):
    whole = held = pltpu.VMEM(fields_now.shape, F32)
    packed = pltpu.VMEM((4, 8, NZ), F32)
    dma = pltpu.SemaphoreType.DMA
    scratch = [
        pltpu.SMEM((3,), jnp.int32), pltpu.VMEM(advect.shape, F32), pltpu.VMEM(diffuse.shape, F32),
        whole, whole, pltpu.VMEM((NX, 24, NY * NZ), F32),
        pltpu.VMEM((4, 64, NY * NZ), BF16), pltpu.VMEM((4, 32, NY * NZ), BF16),
        pltpu.VMEM((GROUPS, 48, 64), BF16), pltpu.VMEM((GROUPS, 48, 32), BF16), pltpu.VMEM((24, 96), F32),
        pltpu.VMEM((NY, 8, NZ), F32), pltpu.VMEM((NY + REACH, 8, NZ), F32), pltpu.VMEM((2, NY, 8, NZ), F32),
        *[pltpu.VMEM((4, NY + REACH, 8, NZ), F32)] * (2 * GROUPS),
        *[pltpu.VMEM((NX, NY, 8, NZ), F32)] * GROUPS,
        *[pltpu.VMEM((REACH, NY, 8, NZ), F32)] * GROUPS,
        *[pltpu.VMEM((14, 14, 8, NZ), F32)] * GROUPS,
        *[packed] * (3 * GROUPS),
        dma((7,)), dma((GROUPS, 2)), dma((GROUPS, 2)), dma((GROUPS,)), dma((GROUPS,)),
        dma((3,)), dma((3,)), dma((GROUPS, 10)), dma((GROUPS, 10)),
    ]
    hbm = pl.BlockSpec(memory_space=pl.ANY)
    return pl.pallas_call(
        kernel,
        out_shape=(held, held),
        in_specs=[pl.BlockSpec(memory_space=pltpu.HBM)] + [hbm] * 4,
        out_specs=(pl.BlockSpec(memory_space=pltpu.VMEM),) * 2,
        scratch_shapes=scratch,
        compiler_params=pltpu.CompilerParams(collective_id=0, has_side_effects=True),
        name="section",
    )(box_shift, fields_now, parent, advect, diffuse)


def out_kernel(slope, value, slope_hbm, value_hbm, sem):
    copies = [pltpu.make_async_copy(slope, slope_hbm, sem.at[0]), pltpu.make_async_copy(value, value_hbm, sem.at[1])]
    for copy in copies:
        copy.start()
    for copy in copies:
        copy.wait()


def hand_out(slope, value):
    shape = jax.ShapeDtypeStruct(slope.shape, F32)
    hbm = pl.BlockSpec(memory_space=pl.ANY)
    slope, value = [pltpu.with_memory_space_constraint(a, pltpu.VMEM) for a in (slope, value)]
    return pl.pallas_call(
        out_kernel, out_shape=(shape, shape), in_specs=[hbm] * 2, out_specs=(hbm, hbm),
        scratch_shapes=[pltpu.SemaphoreType.DMA((2,))], name="out")(slope, value)


def local(fields_now, parent, advect, diffuse, box_shift):
    return hand_out(*section(fields_now, parent, advect, diffuse, box_shift))


def solution(mesh):
    return jax.shard_map(
        local,
        mesh=mesh,
        in_specs=(P(None, "gx", "gy", "gz"), P(None, "gx", "gy", "gz"), P(), P(), P()),
        out_specs=(P(None, "gx", "gy", "gz"), P(None, "gx", "gy", "gz")),
        check_vma=False,
    )
```

profile of v0, /device:TPU:99, one launch (start us, length us, event | category | flops | bytes accessed | tf_op | source)
XLA Modules:
  0.0 35.4 jit_solution(15185480883374392111)
XLA Ops:
  0.6 33.6 %section.1 = (f32[24,8,8,128]{3,2,1,0:T(8,128)S(1)}, f32[24,8,8,128]{3,2,1,0:T(8,128)S(1)}) custom-call(s32[3]{0:T(128)} %shift_hbm.1, f32[24,8,8,128]{3,2,1,0:T(8,128)} %now_hbm.1, f32[24,8,8,128]{3,2,1,0:T(8,128)} %parent_hbm.1, f32[3,24,24]{2,1,0:T(8,128)} %advect_hbm.1, f32[3,24,24]{2,1,0:T(8,128)} %diffuse_hbm.1), custom_call_target="tpu_custom_call" | custom-call | tf_op jit(solution)/shard_map/section/pallas_call | solution.py:371
  34.3 1.2 %out.1 = (f32[24,8,8,128]{3,2,1,0:T(8,128)}, f32[24,8,8,128]{3,2,1,0:T(8,128)}) custom-call(f32[24,8,8,128]{3,2,1,0:T(8,128)S(1)} %get-tuple-element.4.slope, f32[24,8,8,128]{3,2,1,0:T(8,128)S(1)} %get-tuple-element.5.value), custom_call_target="tpu_custom_call" | custom-call | tf_op jit(solution)/shard_map/out/pallas_call | solution.py:394
where the time goes:
time: 35.8 us; the launch traced here: 35.4 us
  Pallas kernels  34.8 us (97%)
  between operations  0.64 us (2%)
    pallas_call x1, Pallas kernels, section(): pl.pallas_call(kernel, out_shape=(held, held), in_specs=[pl.BlockSpec(mem...  33.6 us
    pallas_call x1, Pallas kernels, hand_out(): pl.pallas_call(out_kernel, out_shape=(shape, shape), in_specs=[hbm] * 2,...  1.16 us

commit v1 on v0

--- a/solution.py
+++ b/solution.py
@@ -82,7 +82,11 @@
             packed = [jnp.where(four == at, pltpu.roll(tiles[y], 4 * at, 1), packed[y]) for y in range(NY)]
         return packed
 
-    packed = turn(0, [zero] * NY)
+    packed = [zero] * NY
+    for c in range(GROUPS):
+        packed = turn(c, packed)
+    for y in range(NY):
+        lanes_out[y] = packed[y]
 
     pl.semaphore_wait(barrier, sum(exists(step).astype(jnp.int32) for step in steps))
 
@@ -97,23 +101,15 @@
                         a_send.at[c, h], a_recv.at[c, h], (0, -1, 0)) for h in range(2)] for c in range(GROUPS)]
     b_copies = [remote(moved[c].at[0:REACH], above[c], b_send.at[c], b_recv.at[c], (-1, 0, 0))
                 for c in range(GROUPS)]
-    def send_rows(c):
-        @pl.when(exists((0, -1, 0)))
-        def _():
-            for h in range(2):
-                a_copies[c][h].start()
-
-    send_rows(0)
-    for c in range(1, GROUPS):
-        packed = turn(c, packed)
-    for y in range(NY):
-        lanes_out[y] = packed[y]
     for k in range(2):
         @pl.when(lane_sent[k])
         def _():
             lane_copies[k].start()
-    for c in range(1, GROUPS):
-        send_rows(c)
+    @pl.when(exists((0, -1, 0)))
+    def _():
+        for h in range(2):
+            for c in range(GROUPS):
+                a_copies[c][h].start()
 
     edges = (
         ((-1, 0, 0), lambda c: box[c].at[0:3, 3:11]), ((1, 0, 0), lambda c: box[c].at[11:14, 3:11]),
@@ -216,8 +212,8 @@
         def _():
             b_copies[c].start()
 
-    send_layers(0)
-    take_rows(0, 1)
+    for c in range(GROUPS):
+        send_layers(c)
     for k in range(2):
         @pl.when(lane_received[k])
         def _():
@@ -228,9 +224,7 @@
     @pl.when(lane_sent[2])
     def _():
         lane_copies[2].start()
-    build(0, 0)
-    for c in range(1, GROUPS):
-        send_layers(c)
+    for c in range(GROUPS):
         take_rows(c, 1)
         build(c, 0)
 

time: 35.8 us -> 35.5 us (level)
  no operation moved by 1% of the time
where the time goes in v1:
time: 35.5 us; the launch traced here: 35.2 us
  Pallas kernels  34.5 us (97%)
  between operations  0.64 us (2%)
    pallas_call x1, Pallas kernels, section(): pl.pallas_call(kernel, out_shape=(held, held), in_specs=[pl.BlockSpec(mem...  33.4 us
    pallas_call x1, Pallas kernels, hand_out(): pl.pallas_call(out_kernel, out_shape=(shape, shape), in_specs=[hbm] * 2,...  1.16 us

profile of v1, /device:TPU:99, one launch (start us, length us, event | category | flops | bytes accessed | tf_op | source)
XLA Modules:
  0.0 35.2 jit_solution(15554081983794639950)
XLA Ops:
  0.6 33.4 %section.1 = (f32[24,8,8,128]{3,2,1,0:T(8,128)S(1)}, f32[24,8,8,128]{3,2,1,0:T(8,128)S(1)}) custom-call(s32[3]{0:T(128)} %shift_hbm.1, f32[24,8,8,128]{3,2,1,0:T(8,128)} %now_hbm.1, f32[24,8,8,128]{3,2,1,0:T(8,128)} %parent_hbm.1, f32[3,24,24]{2,1,0:T(8,128)} %advect_hbm.1, f32[3,24,24]{2,1,0:T(8,128)} %diffuse_hbm.1), custom_call_target="tpu_custom_call" | custom-call | tf_op jit(solution)/shard_map/section/pallas_call | solution.py:365
  34.0 1.2 %out.1 = (f32[24,8,8,128]{3,2,1,0:T(8,128)}, f32[24,8,8,128]{3,2,1,0:T(8,128)}) custom-call(f32[24,8,8,128]{3,2,1,0:T(8,128)S(1)} %get-tuple-element.4.slope, f32[24,8,8,128]{3,2,1,0:T(8,128)S(1)} %get-tuple-element.5.value), custom_call_target="tpu_custom_call" | custom-call | tf_op jit(solution)/shard_map/out/pallas_call | solution.py:388

commit v2 on v1

--- a/solution.py
+++ b/solution.py
@@ -70,7 +70,7 @@
         load.start()
 
     lane = lax.broadcasted_iota(jnp.int32, (8, NZ), 1)
-    four, eight = lane // 4, lane // 8
+    four = lane // 4
     zero = jnp.zeros((8, NZ), F32)
 
     def turn(c, packed):
@@ -142,12 +142,11 @@
 
     def arms_of(c, h):
         xs = slice(3 + 4 * h, 7 + 4 * h)
-        pair = slice(2 * h, 2 * h + 2)
         found = [
             (arm(c, 5 * h + 0, box[c].at[xs, 3:6], box[c].at[xs, 11:14], (0, -1, 0)), (0, -1, 0)),
             (arm(c, 5 * h + 1, box[c].at[xs, 8:11], box[c].at[xs, 0:3], (0, 1, 0)), (0, 1, 0)),
-            (arm(c, 5 * h + 2, arm_out[c].at[pair], arm_high[c].at[pair], (0, 0, -1)), (0, 0, -1)),
-            (arm(c, 5 * h + 3, arm_out[c].at[pair], arm_low[c].at[pair], (0, 0, 1)), (0, 0, 1))]
+            (arm(c, 5 * h + 2, arm_out[c].at[h], arm_high[c].at[h], (0, 0, -1)), (0, 0, -1)),
+            (arm(c, 5 * h + 3, arm_out[c].at[2 + h], arm_low[c].at[h], (0, 0, 1)), (0, 0, 1))]
         if h == 0:
             found.append((arm(c, 4, box[c].at[3:6, 3:11], box[c].at[11:14, 3:11], (-1, 0, 0)), (-1, 0, 0)))
         else:
@@ -163,8 +162,8 @@
                 copy.start()
 
     def build(c, h):
+        first_lanes = last_lanes = zero
         for pair in range(2):
-            packed = zero
             for x2 in range(2):
                 x = 4 * h + 2 * pair + x2
                 parent_tiles = jnp.swapaxes(parent_v[8 * c:8 * c + 8, x], 0, 1)
@@ -189,9 +188,11 @@
                     limit = jnp.where(inside, sizes[2] * NZ - gz * NZ - s2, 0)
                     tile = jnp.where(lane < limit, tile, parent_tiles[y])
                     box[c][3 + x, 3 + y] = tile
-                    at = 8 * x2 + y
-                    packed = jnp.where(eight == at, pltpu.roll(tile, (8 * at + 4) % NZ, 1), packed)
-            arm_out[c][2 * h + pair] = packed
+                    at = 16 * pair + 8 * x2 + y
+                    first_lanes = jnp.where(four == at, pltpu.roll(tile, 4 * at, 1), first_lanes)
+                    last_lanes = jnp.where(four == at, pltpu.roll(tile, (4 * at + 4) % NZ, 1), last_lanes)
+        arm_out[c][h] = first_lanes
+        arm_out[c][2 + h] = last_lanes
         send_arms(arms[c][h][2:4] + arms[c][h][0:2])
 
     def shift_y(c, h):
@@ -262,11 +263,12 @@
         return product[0:24] + product[24:48]
 
     def along_xz(c, x, h, pair, x2, slot):
-        ends_pack = jnp.where(lane % 8 < 4, arm_low[c][2 * h + pair], arm_high[c][2 * h + pair])
+        low_pack, high_pack = arm_low[c][h], arm_high[c][h]
         for y in range(NY):
-            at = 8 * x2 + y
+            at = 16 * pair + 8 * x2 + y
             u0 = box[c][3 + x, 3 + y]
-            ends = pltpu.roll(ends_pack, (2 * NZ - 8 * at - 4) % NZ, 1)
+            ends = jnp.where(lane < 64, pltpu.roll(high_pack, (NZ - 4 * at) % NZ, 1),
+                             pltpu.roll(low_pack, (2 * NZ - 4 - 4 * at) % NZ, 1))
             before = [pltpu.roll(jnp.where(lane >= NZ - o, ends, u0), o, 1) for o in (3, 2, 1)]
             after = [pltpu.roll(jnp.where(lane < o, ends, u0), NZ - o, 1) for o in (1, 2, 3)]
             middle = 1.875 * u0

time: 35.5 us -> 35.5 us (level)
  no operation moved by 1% of the time
where the time goes in v2:
time: 35.5 us; the launch traced here: 35.3 us
  Pallas kernels  34.7 us (98%)
  between operations  0.64 us (2%)
    pallas_call x1, Pallas kernels, section(): pl.pallas_call(kernel, out_shape=(held, held), in_specs=[pl.BlockSpec(mem...  33.5 us
    pallas_call x1, Pallas kernels, hand_out(): pl.pallas_call(out_kernel, out_shape=(shape, shape), in_specs=[hbm] * 2,...  1.16 us

profile of v2, /device:TPU:99, one launch (start us, length us, event | category | flops | bytes accessed | tf_op | source)
XLA Modules:
  0.0 35.3 jit_solution(13665699834008528486)
XLA Ops:
  0.6 33.5 %section.1 = (f32[24,8,8,128]{3,2,1,0:T(8,128)S(1)}, f32[24,8,8,128]{3,2,1,0:T(8,128)S(1)}) custom-call(s32[3]{0:T(128)} %shift_hbm.1, f32[24,8,8,128]{3,2,1,0:T(8,128)} %now_hbm.1, f32[24,8,8,128]{3,2,1,0:T(8,128)} %parent_hbm.1, f32[3,24,24]{2,1,0:T(8,128)} %advect_hbm.1, f32[3,24,24]{2,1,0:T(8,128)} %diffuse_hbm.1), custom_call_target="tpu_custom_call" | custom-call | tf_op jit(solution)/shard_map/section/pallas_call | solution.py:367
  34.1 1.2 %out.1 = (f32[24,8,8,128]{3,2,1,0:T(8,128)}, f32[24,8,8,128]{3,2,1,0:T(8,128)}) custom-call(f32[24,8,8,128]{3,2,1,0:T(8,128)S(1)} %get-tuple-element.4.slope, f32[24,8,8,128]{3,2,1,0:T(8,128)S(1)} %get-tuple-element.5.value), custom_call_target="tpu_custom_call" | custom-call | tf_op jit(solution)/shard_map/out/pallas_call | solution.py:390
